TPU v7x, 32 devices: a whole 2x2x4 slice. The times are simulated.
32 devices in a mesh: dp: 4 (over y, core), expert: 8 (over z, x).
Axes of the slice: x: 2, y: 2, z: 4, core: 2. Of those that a mesh axis runs over, the one named last changes fastest.
Arguments:
- tokens: bfloat16 [4096, 1024], P(('dp', 'expert')), may hold values from -6 to 6
- chosen_expert_index: int32 [4096, 6], P(('dp', 'expert')), may hold values from 0 to 7, as said below
- router_gate_weight: float32 [4096, 6], P(('dp', 'expert')), may hold values from 0.05 to 0.5
- output_gradient: bfloat16 [4096, 1024], P(('dp', 'expert')), may hold values from -0.15917969 to 0.15917969
- gate_weight_matrix: bfloat16 [8, 1024, 704], P('expert'), may hold values from -0.1875 to 0.1875
- up_weight: bfloat16 [8, 1024, 704], P('expert'), may hold values from -0.1875 to 0.1875
- down_weight: bfloat16 [8, 704, 1024], P('expert'), may hold values from -0.21875 to 0.21875
- adapter_down_maps: bfloat16 [8, 16, 704], P('expert'), may hold values from -0.21875 to 0.21875
- adapter_up_maps: bfloat16 [8, 16, 1024], P('expert'), may hold values from -1.5 to 1.5
Outputs:
- mixed: bfloat16 [4096, 1024], P(('dp', 'expert'))
- grad_in: bfloat16 [8, 16, 704], P('expert')
- grad_out: bfloat16 [8, 16, 1024], P('expert')
Inputs may be any that keep to these rules, and one draw needn't show every extreme that they name: `chosen_expert_index`: each row names 6 different experts. In each aligned block of 128 rows (the rows of one device) no expert is named by more than 126 rows, and one and the same expert, drawn for the whole array, is named by exactly 126 rows of every block. Each row's experts are 6 neighbours in one circular order of all experts, drawn for the whole array.
All inputs are finite; a program needn't handle non-finite values.
Results may differ from a plain program's by a relative error of at most 0.0064.
Values may be sent and summed in bfloat16 or wider, within the bound.
A program may use at most 64 MiB of HBM per device.

v0:
```python
import functools

import jax
import jax.numpy as jnp
from jax import lax
from jax.experimental import pallas as pl
from jax.experimental.pallas import tpu as pltpu
from jax.sharding import PartitionSpec as P

MESH = pl.DeviceIdType.MESH
F32 = jnp.float32
BF16 = jnp.bfloat16


def dot_nt(a, b):
    return lax.dot_general(a, b, (((1,), (1,)), ((), ())), preferred_element_type=F32)


def dot(a, b):
    return jnp.dot(a, b, preferred_element_type=F32)


def kernel(
    n,
    nd,
    tok_h,
    idx_ref,
    w_ref,
    og_ref,
    gw_h,
    uw_h,
    dw_h,
    ad_ref,
    au_ref,
    mixed_ref,
    gin_ref,
    gout_ref,
    tok_all,
    gw,
    uw,
    dw,
    hid_all,
    out_send,
    pair_recv,
    line_send,
    line_recv,
    gate_recv,
    au_all,
    lg_send,
    lg_recv,
    rk_send,
    rk_recv,
    gexp,
    gp_send,
    gp_recv,
    gin_all,
    gout_all,
    acc,
    loc_sem,
    up_s,
    down_s,
    side_s,
    tok_r,
    gate_s,
    gate_r,
    au_s,
    au_r,
    lg_s,
    lg_r,
    rk_s,
    rk_r,
    pair_s,
    pair_r,
    line_s,
    line_r,
    gp_s,
    gp_r,
    gin_s,
    gin_r,
    gout_s,
    gout_r,
):
    me = lax.axis_index("expert")
    rep = lax.axis_index("dp")
    line = 4 if n % 4 == 0 else n
    side = n // line
    at_line = me // side
    at_side = lax.rem(me, side)
    rows = tok_all.shape[1]
    rank = ad_ref.shape[1]
    width = tok_all.shape[2]

    def peer(s):
        return lax.rem(me + s, n)

    def source(s):
        return lax.rem(me + n - s, n)

    def mate(s):
        return lax.rem(rep + s, nd)

    def to_expert(src, dst, s_sem, r_sem, p):
        return pltpu.make_async_remote_copy(
            src_ref=src,
            dst_ref=dst,
            send_sem=s_sem,
            recv_sem=r_sem,
            device_id={"expert": p},
            device_id_type=MESH,
        )

    def to_mate(src, dst, s_sem, r_sem, p):
        return pltpu.make_async_remote_copy(
            src_ref=src,
            dst_ref=dst,
            send_sem=s_sem,
            recv_sem=r_sem,
            device_id={"dp": p},
            device_id_type=MESH,
        )

    def each(lo, hi, fn):
        def body(s, carry):
            fn(s)
            return carry

        lax.fori_loop(lo, hi, body, 0)

    load_tok = pltpu.make_async_copy(tok_h, tok_all.at[me], loc_sem.at[0])
    load_gw = pltpu.make_async_copy(gw_h.at[0], gw, loc_sem.at[1])
    load_uw = pltpu.make_async_copy(uw_h.at[0], uw, loc_sem.at[2])
    load_dw = pltpu.make_async_copy(dw_h.at[0], dw, loc_sem.at[3])
    load_tok.start()
    load_gw.start()
    load_uw.start()
    load_dw.start()

    eye = lax.broadcasted_iota(jnp.int32, (rows, rows), 0) == lax.broadcasted_iota(
        jnp.int32, (rows, rows), 1
    )

    def spread_gates(e):
        row = jnp.sum(jnp.where(idx_ref[...] == e, w_ref[...], 0.0), axis=0, keepdims=True)
        gexp[e] = jnp.broadcast_to(row, (rank, rows))

    each(0, n, spread_gates)

    barrier = pltpu.get_barrier_semaphore()
    each(
        1,
        n,
        lambda s: pl.semaphore_signal(
            barrier, inc=1, device_id={"expert": peer(s)}, device_id_type=MESH
        ),
    )
    each(
        1,
        nd,
        lambda s: pl.semaphore_signal(
            barrier, inc=1, device_id={"dp": mate(s)}, device_id_type=MESH
        ),
    )
    pl.semaphore_wait(barrier, n - 1 + nd - 1)

    def au_copy(s):
        p = peer(s)
        return to_expert(au_ref.at[0], au_all.at[me], au_s.at[p], au_r.at[me], p)

    def up_copy(z):
        k = z * side + at_side
        p = (at_line + 1) * side + at_side
        return to_expert(tok_all.at[k], tok_all.at[k], up_s.at[z], tok_r.at[k], p)

    def down_copy(z):
        k = z * side + at_side
        p = (at_line - 1) * side + at_side
        return to_expert(tok_all.at[k], tok_all.at[k], down_s.at[z], tok_r.at[k], p)

    def side_copy(z, s):
        k = z * side + at_side
        x = lax.rem(at_side + s, side)
        p = at_line * side + x
        return to_expert(tok_all.at[k], tok_all.at[k], side_s.at[z * side + x], tok_r.at[k], p)

    def gate_copy(s):
        p = peer(s)
        return to_expert(
            gexp.at[p, pl.ds(0, 8)], gate_recv.at[me], gate_s.at[p], gate_r.at[me], p
        )

    def pair_copy(z, x):
        k = z * side + x
        p = at_line * side + x
        return to_expert(
            out_send.at[k], pair_recv.at[z * side + at_side], pair_s.at[k],
            pair_r.at[z * side + at_side], p,
        )

    def line_copy(z):
        p = z * side + at_side
        return to_expert(
            line_send.at[z], line_recv.at[at_line], line_s.at[z], line_r.at[at_line], p
        )

    def lg_copy(s):
        p = peer(s)
        return to_expert(lg_send.at[p], lg_recv.at[me], lg_s.at[p], lg_r.at[me], p)

    def rk_copy(p):
        return to_expert(rk_send.at[p], rk_recv.at[me], rk_s.at[p], rk_r.at[me], p)

    def gp_copy(p):
        return to_expert(gp_send.at[p], gp_recv.at[me], gp_s.at[p], gp_r.at[me], p)

    def gin_copy(s):
        p = mate(s)
        return to_mate(gin_all.at[rep], gin_all.at[rep], gin_s.at[p], gin_r.at[rep], p)

    def gout_copy(s):
        p = mate(s)
        return to_mate(gout_all.at[rep], gout_all.at[rep], gout_s.at[p], gout_r.at[rep], p)

    def arrived(buf, sems, p):
        to_expert(buf.at[p], buf.at[p], sems.at[p], sems.at[p], p).wait_recv()

    def arrived_mate(buf, sems, p):
        to_mate(buf.at[p], buf.at[p], sems.at[p], sems.at[p], p).wait_recv()

    load_tok.wait()

    def spread(z, go_up, go_down):
        @pl.when(go_up & (at_line + 1 < line))
        def _():
            up_copy(z).start()

        @pl.when(go_down & (at_line >= 1))
        def _():
            down_copy(z).start()

        each(1, side, lambda s: side_copy(z, s).start())

    spread(at_line, True, True)
    each(1, n, lambda s: gate_copy(s).start())
    each(1, n, lambda s: au_copy(s).start())
    au_all[me] = au_ref[0]
    gate_recv[me] = gexp[me, 0:8]

    load_gw.wait()
    load_uw.wait()
    load_dw.wait()

    def expert_block(src):
        x = tok_all[src]
        g = dot_nt(x, gw[...])
        u = dot_nt(x, uw[...])
        h = (g / (1.0 + jnp.exp(-g)) * u).astype(BF16)
        hid_all[src] = h
        low_t = dot_nt(ad_ref[0], h).astype(BF16)
        low = dot_nt(h, ad_ref[0]).astype(BF16)
        out = (dot(h, dw[...]) + dot(low, au_ref[0])).astype(BF16)
        return low_t, out

    def low_grads():
        each(1, n, lambda s: arrived(au_all, au_r, source(s)))
        low_grad = dot_nt(au_all[...].reshape(n * rank, width), og_ref[...])
        low_grad = low_grad * gexp[...].reshape(n * rank, rows)
        lg_send[...] = low_grad.astype(BF16).reshape(n, rank, rows)
        lg_recv[me] = lg_send[me]
        each(1, n, lambda s: lg_copy(s).start())

    def on_line(z):
        return (z >= 0) & (z < line)

    def relay(k):
        for sign in (-1, 1):
            z = at_line + sign * k

            @pl.when((k >= 1) & on_line(z))
            def _():
                arrived(tok_all, tok_r, z * side + at_side)
                spread(z, sign < 0, sign > 0)

    def work(k, j):
        s = j // 2
        sign = 1 - 2 * lax.rem(j, 2)
        far = k - jnp.minimum(s, 1)
        z = at_line + sign * far
        x = lax.rem(at_side + s, side)
        src = z * side + x

        @pl.when(on_line(z) & (far >= 0) & ((far > 0) | (sign > 0)))
        def _():
            @pl.when(s > 0)
            def _():
                arrived(tok_all, tok_r, src)

            @pl.when(src != me)
            def _():
                arrived(gate_recv, gate_r, src)

            low_t, out = expert_block(src)
            row = gate_recv[src, 0:1]
            column = jnp.sum(jnp.where(eye, row, 0.0), axis=1, keepdims=True)
            term = (out.astype(F32) * column).astype(BF16)

            @pl.when(s > 0)
            def _():
                out_send[src] = term

            @pl.when(s == 0)
            def _():
                pair_recv[src] = term

            @pl.when(src == me)
            def _():
                rk_recv[me] = low_t

            @pl.when(src != me)
            def _():
                rk_send[src] = low_t
                rk_copy(src).start()

            @pl.when(s > 0)
            def _():
                pair_copy(z, x).start()

    def pair_sum(z):
        def wait_pair(s):
            arrived(pair_recv, pair_r, z * side + lax.rem(at_side + s, side))

        each(1, side, wait_pair)

        def add(x, total):
            return total + pair_recv[z * side + x].astype(F32)

        return lax.fori_loop(1, side, add, pair_recv[z * side].astype(F32))

    def combine(k):
        for sign in (-1, 1):
            z = at_line + sign * (k - 2)

            @pl.when((k >= 3) & on_line(z))
            def _():
                line_send[z] = pair_sum(z).astype(BF16)
                line_copy(z).start()

    def grads():
        each(1, n, lambda s: arrived(lg_recv, lg_r, source(s)))

        def add_gin(src, total):
            return total + dot(lg_recv[src], hid_all[src])

        gin_all[rep] = lax.fori_loop(0, n, add_gin, jnp.zeros(gin_all.shape[1:], F32))

        each(1, n, lambda s: arrived(rk_recv, rk_r, source(s)))
        low_w = (rk_recv[...].astype(F32) * gexp[...]).astype(BF16).reshape(n * rank, rows)
        gp = dot(low_w, og_ref[...])
        gp_send[...] = gp.astype(BF16).reshape(n, rank, width)
        each(1, nd, lambda s: gin_copy(s).start())
        gp_recv[me] = gp_send[me]
        each(1, n, lambda s: gp_copy(peer(s)).start())

    def step(k):
        relay(k)
        each(0, 2 * side, lambda j: work(k, j))
        pl.when(k == 2)(low_grads)
        pl.when(k == line + 1)(grads)
        combine(k)

    each(0, line + 2, step)

    acc[...] = pair_sum(at_line)
    each(1, n, lambda s: arrived(gp_recv, gp_r, source(s)))
    gout_all[rep] = jnp.sum(gp_recv[...].astype(F32), axis=0)
    each(1, nd, lambda s: gout_copy(s).start())

    def finish(t):
        z = lax.rem(at_line + t, line)
        arrived(line_recv, line_r, z)
        acc[...] += line_recv[z].astype(F32)

    each(1, line, finish)
    mixed_ref[...] = acc[...].astype(BF16)

    each(1, nd, lambda s: arrived_mate(gin_all, gin_r, mate(s)))
    gin_ref[0] = jnp.sum(gin_all[...], axis=0).astype(BF16)
    each(1, nd, lambda s: arrived_mate(gout_all, gout_r, mate(s)))
    gout_ref[0] = jnp.sum(gout_all[...], axis=0).astype(BF16)

    def drain(s):
        au_copy(s).wait_send()
        gate_copy(s).wait_send()
        lg_copy(s).wait_send()
        p = peer(s)
        rk_copy(p).wait_send()
        gp_copy(p).wait_send()

    each(1, n, drain)

    def drain_line(z):
        @pl.when((z <= at_line) & (at_line + 1 < line))
        def _():
            up_copy(z).wait_send()

        @pl.when((z >= at_line) & (at_line >= 1))
        def _():
            down_copy(z).wait_send()

        def drain_side(s):
            side_copy(z, s).wait_send()
            pair_copy(z, lax.rem(at_side + s, side)).wait_send()

        each(1, side, drain_side)

        @pl.when(z != at_line)
        def _():
            line_copy(z).wait_send()

    each(0, line, drain_line)

    def drain_mates(s):
        gin_copy(s).wait_send()
        gout_copy(s).wait_send()

    each(1, nd, drain_mates)


def hand_over(a_ref, b_ref, c_ref, x_ref, y_ref, z_ref):
    x_ref[...] = a_ref[...]
    y_ref[...] = b_ref[...]
    z_ref[...] = c_ref[...]


def shards(
    n,
    nd,
    tokens,
    chosen_expert_index,
    router_gate_weight,
    output_gradient,
    gate_weight_matrix,
    up_weight,
    down_weight,
    adapter_down_maps,
    adapter_up_maps,
):
    rows, width = tokens.shape
    rank, hidden = adapter_down_maps.shape[1:]
    line = 4 if n % 4 == 0 else n
    vmem = pl.BlockSpec(memory_space=pltpu.VMEM)
    anywhere = pl.BlockSpec(memory_space=pl.ANY)
    dma = pltpu.SemaphoreType.DMA
    results = pl.pallas_call(
        functools.partial(kernel, n, nd),
        out_shape=(
            jax.ShapeDtypeStruct((rows, width), BF16),
            jax.ShapeDtypeStruct((1, rank, hidden), BF16),
            jax.ShapeDtypeStruct((1, rank, width), BF16),
        ),
        in_specs=[anywhere, vmem, vmem, vmem, anywhere, anywhere, anywhere, vmem, vmem],
        out_specs=(vmem, vmem, vmem),
        scratch_shapes=[
            pltpu.VMEM((n, rows, width), BF16),
            pltpu.VMEM((hidden, width), BF16),
            pltpu.VMEM((hidden, width), BF16),
            pltpu.VMEM((hidden, width), BF16),
            pltpu.VMEM((n, rows, hidden), BF16),
            pltpu.VMEM((n, rows, width), BF16),
            pltpu.VMEM((n, rows, width), BF16),
            pltpu.VMEM((line, rows, width), BF16),
            pltpu.VMEM((line, rows, width), BF16),
            pltpu.VMEM((n, 8, rows), F32),
            pltpu.VMEM((n, rank, width), BF16),
            pltpu.VMEM((n, rank, rows), BF16),
            pltpu.VMEM((n, rank, rows), BF16),
            pltpu.VMEM((n, rank, rows), BF16),
            pltpu.VMEM((n, rank, rows), BF16),
            pltpu.VMEM((n, rank, rows), F32),
            pltpu.VMEM((n, rank, width), BF16),
            pltpu.VMEM((n, rank, width), BF16),
            pltpu.VMEM((nd, rank, hidden), F32),
            pltpu.VMEM((nd, rank, width), F32),
            pltpu.VMEM((rows, width), F32),
            dma((4,)),
        ]
        + [dma((line,))] * 2
        + [dma((n,))] * 12
        + [dma((line,))] * 2
        + [dma((n,))] * 2
        + [dma((nd,))] * 4,
        compiler_params=pltpu.CompilerParams(
            collective_id=0, has_side_effects=True, vmem_limit_bytes=60 * 1024 * 1024
        ),
    )(
        tokens,
        chosen_expert_index.T,
        router_gate_weight.T,
        output_gradient,
        jnp.swapaxes(gate_weight_matrix, 1, 2),
        jnp.swapaxes(up_weight, 1, 2),
        down_weight,
        adapter_down_maps,
        adapter_up_maps,
    )
    return pl.pallas_call(
        hand_over,
        out_shape=tuple(jax.ShapeDtypeStruct(r.shape, r.dtype) for r in results),
        in_specs=[vmem] * 3,
        out_specs=(vmem,) * 3,
    )(*results)


def solution(mesh):
    return jax.shard_map(
        functools.partial(shards, mesh.shape["expert"], mesh.shape["dp"]),
        mesh=mesh,
        in_specs=(
            P(("dp", "expert"), None),
            P(("dp", "expert"), None),
            P(("dp", "expert"), None),
            P(("dp", "expert"), None),
            P("expert", None, None),
            P("expert", None, None),
            P("expert", None, None),
            P("expert", None, None),
            P("expert", None, None),
        ),
        out_specs=(P(("dp", "expert"), None), P("expert", None, None), P("expert", None, None)),
        check_vma=False,
    )
```

profile of v0, /device:TPU:0, one launch (start us, length us, event | category | flops | bytes accessed | tf_op | source)
XLA Modules:
  0.0 87.0 jit_solution(8299578758096478409)
XLA Ops:
  0.6 84.6 %shard_map.112 = (bf16[128,1024]{1,0:T(8,128)(2,1)}, bf16[1,16,704]{2,1,0:T(8,128)(2,1)}, bf16[1,16,1024]{2,1,0:T(8,128)(2,1)}) custom-call(bf16[128,1024]{1,0:T(8,128)(2,1)} %tok_h.1, s32[6,128]{1,0:T(8,128)} %bitcast.6, f32[6,128]{1,0:T(8,128)} %bitcast.7, bf16[128,1024]{1,0:T(8,128)(2,1)} %og_ref.1, bf16[1,704,1024]{2,1,0:T(8,128)(2,1)} %bitcast.4, ...), custom_call_target="tpu_custom_call" | custom-call | tf_op jit(solution)/shard_map/pallas_call | solution.py:453
  85.3 1.7 %shard_map.113 = (bf16[128,1024]{1,0:T(8,128)(2,1)}, bf16[1,16,704]{2,1,0:T(8,128)(2,1)}, bf16[1,16,1024]{2,1,0:T(8,128)(2,1)}) custom-call(bf16[128,1024]{1,0:T(8,128)(2,1)} %get-tuple-element.6.a_ref, bf16[1,16,704]{2,1,0:T(8,128)(2,1)} %get-tuple-element.7.b_ref, bf16[1,16,1024]{2,1,0:T(8,128)(2,1)} %get-tuple-element.8.c_ref), custom_call_target="tpu_custom_call" | custom-call | tf_op jit(solution)/shard_map/pallas_call | solution.py:505
where the time goes:
time: 87.1 us; the launch traced here: 87 us
  Pallas kernels  86.3 us (99%)
    pallas_call x1, Pallas kernels, shards(): pl.pallas_call(functools.partial(kernel, n, nd), out_shape=(jax.ShapeDtyp...  84.6 us

commit v1 on v0

v1 whole, which is shorter than its diff:
```python
import functools

import jax
import jax.numpy as jnp
from jax import lax
from jax.experimental import pallas as pl
from jax.experimental.pallas import tpu as pltpu
from jax.sharding import PartitionSpec as P

MESH = pl.DeviceIdType.MESH
F32 = jnp.float32
BF16 = jnp.bfloat16
CHUNKS = 2


def dot_nt(a, b):
    return lax.dot_general(a, b, (((1,), (1,)), ((), ())), preferred_element_type=F32)


def dot(a, b):
    return jnp.dot(a, b, preferred_element_type=F32)


def each(lo, hi, fn):
    def body(s, carry):
        fn(s)
        return carry

    lax.fori_loop(lo, hi, body, 0)


def line_of(n):
    return 4 if n % 4 == 0 else n


def parts_of(nd, width):
    parts = 1
    while parts * 2 <= nd and width % (parts * 2 * 128) == 0:
        parts *= 2
    return parts


def kernel(
    n,
    nd,
    tok_h,
    idx_ref,
    w_ref,
    og_ref,
    gw_h,
    uw_h,
    dw_h,
    ad_ref,
    au_h,
    mixed_ref,
    gin_ref,
    gout_ref,
    tok_all,
    gw,
    uw,
    dw,
    hid_all,
    term,
    pair_recv,
    near_recv,
    line_send,
    line_recv,
    gate_recv,
    au_all,
    lg_send,
    lg_recv,
    rk_send,
    rk_recv,
    gexp,
    gp_buf,
    gm_recv,
    ge_send,
    ge_recv,
    go_buf,
    gin_all,
    acc,
    loc_sem,
    up_s,
    down_s,
    side_s,
    tok_r,
    pair_s,
    pair_r,
    near_s,
    near_r,
    line_s,
    line_r,
    gate_s,
    gate_r,
    au_s,
    au_r,
    am_s,
    am_r,
    lg_s,
    lg_r,
    rk_s,
    rk_r,
    gm_s,
    gm_r,
    ge_s,
    ge_r,
    go_s,
    go_r,
    gin_s,
    gin_r,
):
    me = lax.axis_index("expert")
    rep = lax.axis_index("dp")
    line = line_of(n)
    side = n // line
    at_line = me // side
    at_side = lax.rem(me, side)
    rows = tok_all.shape[1]
    rank = ad_ref.shape[1]
    width = tok_all.shape[2]
    hidden = ad_ref.shape[2]
    parts = parts_of(nd, width)
    part = width // parts
    cr = rows // CHUNKS
    owner = rep < parts

    def peer(s):
        return lax.rem(me + s, n)

    def mate(s):
        return lax.rem(rep + s, nd)

    def other(s):
        return lax.rem(at_side + s, side)

    def to_expert(src, dst, s_sem, r_sem, p):
        return pltpu.make_async_remote_copy(
            src_ref=src,
            dst_ref=dst,
            send_sem=s_sem,
            recv_sem=r_sem,
            device_id={"expert": p},
            device_id_type=MESH,
        )

    def to_mate(src, dst, s_sem, r_sem, p):
        return pltpu.make_async_remote_copy(
            src_ref=src,
            dst_ref=dst,
            send_sem=s_sem,
            recv_sem=r_sem,
            device_id={"dp": p},
            device_id_type=MESH,
        )

    def on_line(z):
        return (z >= 0) & (z < line)

    def chunk(c):
        return pl.ds(pl.multiple_of(c * cr, cr), cr)

    def cols(p):
        return pl.ds(pl.multiple_of(p * part, part), part)

    loads = [
        pltpu.make_async_copy(tok_h, tok_all.at[me], loc_sem.at[0]),
        pltpu.make_async_copy(gw_h.at[0], gw, loc_sem.at[1]),
        pltpu.make_async_copy(uw_h.at[0], uw, loc_sem.at[2]),
        pltpu.make_async_copy(dw_h.at[0], dw.at[pl.ds(0, hidden)], loc_sem.at[3]),
        pltpu.make_async_copy(au_h.at[0], dw.at[pl.ds(hidden, rank)], loc_sem.at[4]),
    ]
    for load in loads:
        load.start()

    def load_map():
        return pltpu.make_async_copy(
            au_h.at[0, :, cols(rep)], au_all.at[me, :, cols(rep)], loc_sem.at[5]
        )

    @pl.when(owner)
    def _():
        load_map().start()

    barrier = pltpu.get_barrier_semaphore()
    each(
        1,
        n,
        lambda s: pl.semaphore_signal(
            barrier, inc=1, device_id={"expert": peer(s)}, device_id_type=MESH
        ),
    )
    each(
        1,
        nd,
        lambda s: pl.semaphore_signal(
            barrier, inc=1, device_id={"dp": mate(s)}, device_id_type=MESH
        ),
    )

    eye = lax.broadcasted_iota(jnp.int32, (rows, rows), 0) == lax.broadcasted_iota(
        jnp.int32, (rows, rows), 1
    )

    def spread_gates(e):
        row = jnp.sum(jnp.where(idx_ref[...] == e, w_ref[...], 0.0), axis=0, keepdims=True)
        gexp[e] = jnp.broadcast_to(row, (rank, rows))

    each(0, n, spread_gates)
    gate_recv[me] = gexp[me, 0:8]

    def up_copy(z, c):
        k = z * side + at_side
        p = (at_line + 1) * side + at_side
        ref = tok_all.at[k, chunk(c)]
        return to_expert(ref, ref, up_s.at[z, c], tok_r.at[k, c], p)

    def down_copy(z, c):
        k = z * side + at_side
        p = (at_line - 1) * side + at_side
        ref = tok_all.at[k, chunk(c)]
        return to_expert(ref, ref, down_s.at[z, c], tok_r.at[k, c], p)

    def side_copy(z, s, c):
        k = z * side + at_side
        x = other(s)
        p = at_line * side + x
        ref = tok_all.at[k, chunk(c)]
        return to_expert(ref, ref, side_s.at[z * side + x, c], tok_r.at[k, c], p)

    def gate_copy(s):
        p = peer(s)
        return to_expert(
            gexp.at[p, pl.ds(0, 8)], gate_recv.at[me], gate_s.at[p], gate_r.at[me], p
        )

    def au_copy(s):
        p = peer(s)
        ref = au_all.at[me, :, cols(rep)]
        return to_expert(ref, ref, au_s.at[p], au_r.at[me], p)

    def am_copy(s):
        p = mate(s)
        ref = au_all.at[:, :, cols(rep)]
        return to_mate(ref, ref, am_s.at[p], am_r.at[rep], p)

    def pair_copy(z, x, c):
        k = z * side + x
        p = at_line * side + x
        mine = z * side + at_side
        return to_expert(
            term.at[k, chunk(c)], pair_recv.at[mine, chunk(c)], pair_s.at[k, c],
            pair_r.at[mine, c], p,
        )

    def near_copy(z, x):
        b = jnp.where(z > at_line, 0, 1)
        p = z * side + at_side
        return to_expert(
            term.at[z * side + x], near_recv.at[b, x], near_s.at[b, x], near_r.at[b, x], p
        )

    def line_copy(z, c):
        p = z * side + at_side
        return to_expert(
            line_send.at[z, chunk(c)], line_recv.at[at_line, chunk(c)], line_s.at[z, c],
            line_r.at[at_line, c], p,
        )

    def lg_copy(s):
        p = peer(s)
        return to_expert(lg_send.at[p], lg_recv.at[me], lg_s.at[p], lg_r.at[me], p)

    def rk_copy(p):
        return to_expert(rk_send.at[p], rk_recv.at[me], rk_s.at[p], rk_r.at[me], p)

    def gm_copy(s):
        p = mate(s)
        return to_mate(gp_buf.at[:, cols(p)], gm_recv.at[rep], gm_s.at[p], gm_r.at[rep], p)

    def ge_copy(s):
        p = peer(s)
        return to_expert(ge_send.at[p], ge_recv.at[me], ge_s.at[p], ge_r.at[me], p)

    def go_copy(s):
        p = mate(s)
        ref = go_buf.at[:, cols(rep)]
        return to_mate(ref, ref, go_s.at[p], go_r.at[rep], p)

    def gin_copy(s):
        p = mate(s)
        return to_mate(gin_all.at[rep], gin_all.at[rep], gin_s.at[p], gin_r.at[rep], p)

    def arrived(ref, sem):
        to_expert(ref, ref, sem, sem, me).wait_recv()

    def arrived_tok(k, c):
        arrived(tok_all.at[k, chunk(c)], tok_r.at[k, c])

    def spread(z, c, go_up, go_down):
        each(1, side, lambda s: side_copy(z, s, c).start())

        @pl.when(go_up & (at_line + 1 < line))
        def _():
            up_copy(z, c).start()

        @pl.when(go_down & (at_line >= 1))
        def _():
            down_copy(z, c).start()

    loads[0].wait()
    pl.semaphore_wait(barrier, n - 1 + nd - 1)

    each(1, n, lambda s: gate_copy(s).start())
    each(0, CHUNKS, lambda c: spread(at_line, c, True, True))
    for load in loads[1:]:
        load.wait()

    @pl.when(owner)
    def _():
        load_map().wait()
        each(1, n, lambda s: au_copy(s).start())

    def share_maps():
        @pl.when(owner)
        def _():
            def arrived_au(s):
                p = peer(s)
                arrived(au_all.at[p, :, cols(rep)], au_r.at[p])

            each(1, n, arrived_au)
            each(1, nd, lambda s: am_copy(s).start())

    def low_grads():
        def arrived_am(s):
            p = mate(s)

            @pl.when(p < parts)
            def _():
                arrived(au_all.at[:, :, cols(p)], am_r.at[p])

        each(1, nd, arrived_am)
        low_grad = dot_nt(au_all[...].reshape(n * rank, width), og_ref[...])
        low_grad = low_grad * gexp[...].reshape(n * rank, rows)
        lg_send[...] = low_grad.astype(BF16).reshape(n, rank, rows)
        lg_recv[me] = lg_send[me]
        each(1, n, lambda s: lg_copy(s).start())

    def relay(k):
        def piece(c):
            for sign in (-1, 1):
                z = at_line + sign * k

                @pl.when((k >= 1) & on_line(z))
                def _():
                    arrived_tok(z * side + at_side, c)
                    spread(z, c, sign < 0, sign > 0)

        each(0, CHUNKS, piece)

    def expert_block(src):
        x = tok_all[src]
        g = dot_nt(x, gw[...])
        u = dot_nt(x, uw[...])
        h = (g / (1.0 + jnp.exp(-g)) * u).astype(BF16)
        low = dot_nt(h, ad_ref[0])
        hid_all[src, :, 0:hidden] = h
        hid_all[src, :, hidden : hidden + rank] = low.astype(BF16)
        out = dot(hid_all[src], dw[...]).astype(BF16)
        return low.T.astype(BF16), out

    def work(k, j):
        s = j // 2
        sign = 1 - 2 * lax.rem(j, 2)
        far = k - jnp.minimum(s, 1)
        z = at_line + sign * far
        x = other(s)
        src = z * side + x

        @pl.when(on_line(z) & (far >= 0) & ((far > 0) | (sign > 0)))
        def _():
            @pl.when(s > 0)
            def _():
                each(0, CHUNKS, lambda c: arrived_tok(src, c))

            @pl.when(src != me)
            def _():
                arrived(gate_recv.at[src], gate_r.at[src])

            low_t, out = expert_block(src)
            row = gate_recv[src, 0:1]
            column = jnp.sum(jnp.where(eye, row, 0.0), axis=1, keepdims=True)
            term[src] = (out.astype(F32) * column).astype(BF16)

            @pl.when(src == me)
            def _():
                rk_recv[me] = low_t

            @pl.when(src != me)
            def _():
                rk_send[src] = low_t
                rk_copy(src).start()

            @pl.when((s > 0) & (far == 1))
            def _():
                near_copy(z, x).start()

            @pl.when((s > 0) & (far >= 2))
            def _():
                each(0, CHUNKS, lambda c: pair_copy(z, x, c).start())

    def near_own():
        for sign in (-1, 1):
            z = at_line + sign

            @pl.when(on_line(z))
            def _():
                near_copy(z, at_side).start()

    def step(k):
        relay(k)
        pl.when(k == 2)(near_own)
        each(0, 2 * side, lambda j: work(k, j))
        pl.when(k == 1)(share_maps)
        pl.when(k == 2)(low_grads)

    each(0, line + 1, step)

    def pairs(k):
        for sign in (-1, 1):
            z = at_line + sign * k

            @pl.when(on_line(z))
            def _():
                def piece(c):
                    def wait_pair(s):
                        src = z * side + other(s)
                        arrived(pair_recv.at[src, chunk(c)], pair_r.at[src, c])

                    each(1, side, wait_pair)

                    def add(s, total):
                        return total + pair_recv[z * side + other(s), chunk(c)].astype(F32)

                    total = lax.fori_loop(
                        1, side, add, term[z * side + at_side, chunk(c)].astype(F32)
                    )
                    line_send[z, chunk(c)] = total.astype(BF16)
                    line_copy(z, c).start()

                each(0, CHUNKS, piece)

    def near_sum(x, total_ref):
        total_ref[...] = term[at_line * side + x].astype(F32)

        @pl.when(at_line >= 1)
        def _():
            arrived(near_recv.at[0, x], near_r.at[0, x])
            total_ref[...] += near_recv[0, x].astype(F32)

        @pl.when(at_line + 1 < line)
        def _():
            arrived(near_recv.at[1, x], near_r.at[1, x])
            total_ref[...] += near_recv[1, x].astype(F32)

    def merge(s):
        x = other(s)
        near_sum(x, acc)
        term[at_line * side + x] = acc[...].astype(BF16)
        each(0, CHUNKS, lambda c: pair_copy(at_line, x, c).start())

    def in_grads():
        def arrived_lg(s):
            p = peer(s)
            arrived(lg_recv.at[p], lg_r.at[p])

        each(1, n, arrived_lg)

        def add_gin(src, total):
            return total + dot(lg_recv[src], hid_all[src])

        gin_all[rep] = lax.fori_loop(0, n, add_gin, jnp.zeros(gin_all.shape[1:], F32))
        each(1, nd, lambda s: gin_copy(s).start())

    def out_grads():
        def arrived_rk(s):
            p = peer(s)
            arrived(rk_recv.at[p], rk_r.at[p])

        each(1, n, arrived_rk)
        low_w = (rk_recv[...].astype(F32) * gexp[...]).astype(BF16).reshape(n * rank, rows)
        gp_buf[...] = dot(low_w, og_ref[...]).astype(BF16)

        def send(s):
            @pl.when(mate(s) < parts)
            def _():
                gm_copy(s).start()

        each(1, nd, send)

    def mate_sum():
        @pl.when(owner)
        def _():
            def add(s, total):
                p = mate(s)
                arrived(gm_recv.at[p], gm_r.at[p])
                return total + gm_recv[p].astype(F32)

            total = lax.fori_loop(1, nd, add, gp_buf[:, cols(rep)].astype(F32))
            ge_send[...] = total.astype(BF16).reshape(n, rank, part)
            each(1, n, lambda s: ge_copy(s).start())

    def expert_sum():
        @pl.when(owner)
        def _():
            def add(s, total):
                p = peer(s)
                arrived(ge_recv.at[p], ge_r.at[p])
                return total + ge_recv[p].astype(F32)

            total = lax.fori_loop(1, n, add, ge_send[me].astype(F32))
            go_buf[:, cols(rep)] = total.astype(BF16)
            each(1, nd, lambda s: go_copy(s).start())

    in_grads()
    pairs(2)
    out_grads()
    each(1, side, merge)
    for k in range(3, line):
        pairs(k)
    mate_sum()

    near_sum(at_side, acc)

    def add_merged(s):
        src = at_line * side + other(s)
        each(0, CHUNKS, lambda c: arrived(pair_recv.at[src, chunk(c)], pair_r.at[src, c]))
        acc[...] += pair_recv[src].astype(F32)

    each(1, side, add_merged)
    expert_sum()

    for k in range(2, line):
        for sign in (-1, 1):
            z = at_line + sign * k

            @pl.when(on_line(z))
            def _():
                each(
                    0, CHUNKS, lambda c: arrived(line_recv.at[z, chunk(c)], line_r.at[z, c])
                )
                acc[...] += line_recv[z].astype(F32)

    mixed_ref[...] = acc[...].astype(BF16)

    def arrived_gin(s):
        p = mate(s)
        arrived(gin_all.at[p], gin_r.at[p])

    each(1, nd, arrived_gin)
    gin_ref[0] = jnp.sum(gin_all[...], axis=0)[:, 0:hidden].astype(BF16)

    def arrived_go(s):
        p = mate(s)

        @pl.when(p < parts)
        def _():
            arrived(go_buf.at[:, cols(p)], go_r.at[p])

    each(1, nd, arrived_go)
    gout_ref[0] = go_buf[...]

    def drain(s):
        gate_copy(s).wait_send()
        lg_copy(s).wait_send()
        rk_copy(peer(s)).wait_send()

        @pl.when(owner)
        def _():
            au_copy(s).wait_send()
            ge_copy(s).wait_send()

    each(1, n, drain)

    def drain_line(z):
        def piece(c):
            @pl.when((z <= at_line) & (at_line + 1 < line))
            def _():
                up_copy(z, c).wait_send()

            @pl.when((z >= at_line) & (at_line >= 1))
            def _():
                down_copy(z, c).wait_send()

            each(1, side, lambda s: side_copy(z, s, c).wait_send())

            @pl.when((z == at_line) | (z - at_line >= 2) | (at_line - z >= 2))
            def _():
                each(1, side, lambda s: pair_copy(z, other(s), c).wait_send())

            @pl.when((z - at_line >= 2) | (at_line - z >= 2))
            def _():
                line_copy(z, c).wait_send()

        each(0, CHUNKS, piece)

        @pl.when((z - at_line == 1) | (at_line - z == 1))
        def _():
            each(0, side, lambda x: near_copy(z, x).wait_send())

    each(0, line, drain_line)

    def drain_mates(s):
        gin_copy(s).wait_send()

        @pl.when(mate(s) < parts)
        def _():
            gm_copy(s).wait_send()

        @pl.when(owner)
        def _():
            am_copy(s).wait_send()
            go_copy(s).wait_send()

    each(1, nd, drain_mates)


def hand_over(a_ref, b_ref, c_ref, x_ref, y_ref, z_ref):
    x_ref[...] = a_ref[...]
    y_ref[...] = b_ref[...]
    z_ref[...] = c_ref[...]


def shards(
    n,
    nd,
    tokens,
    chosen_expert_index,
    router_gate_weight,
    output_gradient,
    gate_weight_matrix,
    up_weight,
    down_weight,
    adapter_down_maps,
    adapter_up_maps,
):
    rows, width = tokens.shape
    rank, hidden = adapter_down_maps.shape[1:]
    line = line_of(n)
    side = n // line
    parts = parts_of(nd, width)
    part = width // parts
    vmem = pl.BlockSpec(memory_space=pltpu.VMEM)
    anywhere = pl.BlockSpec(memory_space=pl.ANY)
    dma = pltpu.SemaphoreType.DMA
    results = pl.pallas_call(
        functools.partial(kernel, n, nd),
        out_shape=(
            jax.ShapeDtypeStruct((rows, width), BF16),
            jax.ShapeDtypeStruct((1, rank, hidden), BF16),
            jax.ShapeDtypeStruct((1, rank, width), BF16),
        ),
        in_specs=[anywhere, vmem, vmem, vmem, anywhere, anywhere, anywhere, vmem, anywhere],
        out_specs=(vmem, vmem, vmem),
        scratch_shapes=[
            pltpu.VMEM((n, rows, width), BF16),
            pltpu.VMEM((hidden, width), BF16),
            pltpu.VMEM((hidden, width), BF16),
            pltpu.VMEM((hidden + rank, width), BF16),
            pltpu.VMEM((n, rows, hidden + rank), BF16),
            pltpu.VMEM((n, rows, width), BF16),
            pltpu.VMEM((n, rows, width), BF16),
            pltpu.VMEM((2, side, rows, width), BF16),
            pltpu.VMEM((line, rows, width), BF16),
            pltpu.VMEM((line, rows, width), BF16),
            pltpu.VMEM((n, 8, rows), F32),
            pltpu.VMEM((n, rank, width), BF16),
            pltpu.VMEM((n, rank, rows), BF16),
            pltpu.VMEM((n, rank, rows), BF16),
            pltpu.VMEM((n, rank, rows), BF16),
            pltpu.VMEM((n, rank, rows), BF16),
            pltpu.VMEM((n, rank, rows), F32),
            pltpu.VMEM((n * rank, width), BF16),
            pltpu.VMEM((nd, n * rank, part), BF16),
            pltpu.VMEM((n, rank, part), BF16),
            pltpu.VMEM((n, rank, part), BF16),
            pltpu.VMEM((rank, width), BF16),
            pltpu.VMEM((nd, rank, hidden + rank), F32),
            pltpu.VMEM((rows, width), F32),
            dma((6,)),
        ]
        + [dma((line, CHUNKS))] * 2
        + [dma((n, CHUNKS))] * 4
        + [dma((2, side))] * 2
        + [dma((line, CHUNKS))] * 2
        + [dma((n,))] * 4
        + [dma((nd,))] * 2
        + [dma((n,))] * 4
        + [dma((nd,))] * 2
        + [dma((n,))] * 2
        + [dma((nd,))] * 4,
        compiler_params=pltpu.CompilerParams(
            collective_id=0, has_side_effects=True, vmem_limit_bytes=60 * 1024 * 1024
        ),
    )(
        tokens,
        chosen_expert_index.T,
        router_gate_weight.T,
        output_gradient,
        jnp.swapaxes(gate_weight_matrix, 1, 2),
        jnp.swapaxes(up_weight, 1, 2),
        down_weight,
        adapter_down_maps,
        adapter_up_maps,
    )
    return pl.pallas_call(
        hand_over,
        out_shape=tuple(jax.ShapeDtypeStruct(r.shape, r.dtype) for r in results),
        in_specs=[vmem] * 3,
        out_specs=(vmem,) * 3,
    )(*results)


def solution(mesh):
    return jax.shard_map(
        functools.partial(shards, mesh.shape["expert"], mesh.shape["dp"]),
        mesh=mesh,
        in_specs=(
            P(("dp", "expert"), None),
            P(("dp", "expert"), None),
            P(("dp", "expert"), None),
            P(("dp", "expert"), None),
            P("expert", None, None),
            P("expert", None, None),
            P("expert", None, None),
            P("expert", None, None),
            P("expert", None, None),
        ),
        out_specs=(P(("dp", "expert"), None), P("expert", None, None), P("expert", None, None)),
        check_vma=False,
    )
```

time: 87.1 us -> 65.6 us (0.75)
  Pallas kernels: 86.3 us -> 64.8 us
    pallas_call x1, Pallas kernels: 84.6 us -> 63.1 us  [shards(): pl.pallas_call(functools.partial(kernel, n, nd), out_shape=(jax.ShapeDtyp...]
where the time goes in v1:
time: 65.6 us; the launch traced here: 65.4 us
  Pallas kernels  64.8 us (99%)
    pallas_call x1, Pallas kernels, shards(): pl.pallas_call(functools.partial(kernel, n, nd), out_shape=(jax.ShapeDtyp...  63.1 us
    pallas_call x1, Pallas kernels, shards(): pl.pallas_call(hand_over, out_shape=tuple((jax.ShapeDtypeStruct(r.shape,...  1.7 us

profile of v1, /device:TPU:0, one launch (start us, length us, event | category | flops | bytes accessed | tf_op | source)
XLA Modules:
  0.0 65.4 jit_solution(12199015586348432832)
XLA Ops:
  0.6 63.1 %shard_map.112 = (bf16[128,1024]{1,0:T(8,128)(2,1)}, bf16[1,16,704]{2,1,0:T(8,128)(2,1)}, bf16[1,16,1024]{2,1,0:T(8,128)(2,1)}) custom-call(bf16[128,1024]{1,0:T(8,128)(2,1)} %tok_h.1, s32[6,128]{1,0:T(8,128)} %bitcast.6, f32[6,128]{1,0:T(8,128)} %bitcast.7, bf16[128,1024]{1,0:T(8,128)(2,1)} %og_ref.1, bf16[1,704,1024]{2,1,0:T(8,128)(2,1)} %bitcast.4, ...), custom_call_target="tpu_custom_call" | custom-call | tf_op jit(solution)/shard_map/pallas_call | solution.py:655
  63.7 1.7 %shard_map.113 = (bf16[128,1024]{1,0:T(8,128)(2,1)}, bf16[1,16,704]{2,1,0:T(8,128)(2,1)}, bf16[1,16,1024]{2,1,0:T(8,128)(2,1)}) custom-call(bf16[128,1024]{1,0:T(8,128)(2,1)} %get-tuple-element.6.a_ref, bf16[1,16,704]{2,1,0:T(8,128)(2,1)} %get-tuple-element.7.b_ref, bf16[1,16,1024]{2,1,0:T(8,128)(2,1)} %get-tuple-element.8.c_ref), custom_call_target="tpu_custom_call" | custom-call | tf_op jit(solution)/shard_map/pallas_call | solution.py:715

commit v2 on v1

--- a/solution.py
+++ b/solution.py
@@ -30,7 +30,13 @@
 
 
 def line_of(n):
-    return 4 if n % 4 == 0 else n
+    assert n % 4 == 0
+    return 4
+
+
+OUTER = ((0, 0), (1, 0), (0, 1), (2, 0), (1, 1), (2, 1), (3, 0), (3, 1))
+INNER = ((0, 0), (1, 0), (-1, 0), (0, 1), (1, 1), (-1, 1), (2, 1), (2, 0))
+RELAYS = {1: ((1, 0), (1, 1)), 2: ((2, 0),), 3: ((2, 1),), 5: ((3, 0), (3, 1))}
 
 
 def parts_of(nd, width):
@@ -83,6 +89,7 @@
     up_s,
     down_s,
     side_s,
+    onward_s,
     tok_r,
     pair_s,
     pair_r,
@@ -123,6 +130,8 @@
     part = width // parts
     cr = rows // CHUNKS
     owner = rep < parts
+    front = jnp.where(2 * at_line < line, 1, -1)
+    outer = (at_line == 0) | (at_line == line - 1)
 
     def peer(s):
         return lax.rem(me + s, n)
@@ -206,7 +215,7 @@
         gexp[e] = jnp.broadcast_to(row, (rank, rows))
 
     each(0, n, spread_gates)
-    gate_recv[me] = gexp[me, 0:8]
+    gate_recv[me] = gexp[me, 0:1]
 
     def up_copy(z, c):
         k = z * side + at_side
@@ -227,10 +236,16 @@
         ref = tok_all.at[k, chunk(c)]
         return to_expert(ref, ref, side_s.at[z * side + x, c], tok_r.at[k, c], p)
 
+    def onward_copy(s, c):
+        x = other(s)
+        ref = tok_all.at[at_line * side + x, chunk(c)]
+        p = (at_line + front) * side + at_side
+        return to_expert(ref, ref, onward_s.at[x, c], tok_r.at[at_line * side + x, c], p)
+
     def gate_copy(s):
         p = peer(s)
         return to_expert(
-            gexp.at[p, pl.ds(0, 8)], gate_recv.at[me], gate_s.at[p], gate_r.at[me], p
+            gexp.at[p, pl.ds(0, 1)], gate_recv.at[me], gate_s.at[p], gate_r.at[me], p
         )
 
     def au_copy(s):
@@ -296,8 +311,13 @@
     def arrived_tok(k, c):
         arrived(tok_all.at[k, chunk(c)], tok_r.at[k, c])
 
+    def crosses(z):
+        return outer | (z != at_line - front)
+
     def spread(z, c, go_up, go_down):
-        each(1, side, lambda s: side_copy(z, s, c).start())
+        @pl.when(crosses(z))
+        def _():
+            each(1, side, lambda s: side_copy(z, s, c).start())
 
         @pl.when(go_up & (at_line + 1 < line))
         def _():
@@ -315,10 +335,11 @@
     for load in loads[1:]:
         load.wait()
 
-    @pl.when(owner)
-    def _():
-        load_map().wait()
-        each(1, n, lambda s: au_copy(s).start())
+    def send_maps():
+        @pl.when(owner)
+        def _():
+            load_map().wait()
+            each(1, n, lambda s: au_copy(s).start())
 
     def share_maps():
         @pl.when(owner)
@@ -345,17 +366,22 @@
         lg_recv[me] = lg_send[me]
         each(1, n, lambda s: lg_copy(s).start())
 
-    def relay(k):
-        def piece(c):
-            for sign in (-1, 1):
-                z = at_line + sign * k
-
-                @pl.when((k >= 1) & on_line(z))
-                def _():
-                    arrived_tok(z * side + at_side, c)
-                    spread(z, c, sign < 0, sign > 0)
-
-        each(0, CHUNKS, piece)
+    def relay(k, c):
+        for sign in (-1, 1):
+            z = at_line + sign * k
+
+            @pl.when((k >= 1) & on_line(z))
+            def _():
+                arrived_tok(z * side + at_side, c)
+                spread(z, c, sign < 0, sign > 0)
+
+        @pl.when((k == 1) & outer)
+        def _():
+            def onward(s):
+                arrived_tok(at_line * side + other(s), c)
+                onward_copy(s, c).start()
+
+            each(1, side, onward)
 
     def expert_block(src):
         x = tok_all[src]
@@ -368,17 +394,13 @@
         out = dot(hid_all[src], dw[...]).astype(BF16)
         return low.T.astype(BF16), out
 
-    def work(k, j):
-        s = j // 2
-        sign = 1 - 2 * lax.rem(j, 2)
-        far = k - jnp.minimum(s, 1)
-        z = at_line + sign * far
+    def work(dist, s):
+        z = at_line + front * dist
         x = other(s)
         src = z * side + x
 
-        @pl.when(on_line(z) & (far >= 0) & ((far > 0) | (sign > 0)))
-        def _():
-            @pl.when(s > 0)
+        def run():
+            @pl.when((s > 0) & ((dist != 0) | ~outer))
             def _():
                 each(0, CHUNKS, lambda c: arrived_tok(src, c))
 
@@ -400,38 +422,54 @@
                 rk_send[src] = low_t
                 rk_copy(src).start()
 
-            @pl.when((s > 0) & (far == 1))
+            @pl.when((s > 0) & ((dist == 1) | (dist == -1)))
             def _():
                 near_copy(z, x).start()
 
-            @pl.when((s > 0) & (far >= 2))
+            @pl.when((s > 0) & (dist >= 2))
             def _():
                 each(0, CHUNKS, lambda c: pair_copy(z, x, c).start())
 
-    def near_own():
-        for sign in (-1, 1):
-            z = at_line + sign
-
-            @pl.when(on_line(z))
-            def _():
-                near_copy(z, at_side).start()
-
-    def step(k):
-        relay(k)
-        pl.when(k == 2)(near_own)
-        each(0, 2 * side, lambda j: work(k, j))
-        pl.when(k == 1)(share_maps)
-        pl.when(k == 2)(low_grads)
-
-    each(0, line + 1, step)
-
-    def pairs(k):
+        run()
+
+    def near_own(z):
+        @pl.when(on_line(z))
+        def _():
+            near_copy(z, at_side).start()
+
+    def pick(i, values):
+        total = 0
+        for j, value in enumerate(values):
+            total = total + value * (i == j).astype(jnp.int32)
+        return total
+
+    def step(i):
+        for at, pieces in RELAYS.items():
+
+            @pl.when(i == at)
+            def _():
+                for k, c in pieces:
+                    relay(k, c)
+
+        pl.when(i == 3)(lambda: near_own(at_line + front))
+        pl.when(i == 5)(lambda: near_own(at_line - front))
+        inner = 1 - outer.astype(jnp.int32)
+        dist = pick(i, [d for d, _ in OUTER]) * (1 - inner) + pick(i, [d for d, _ in INNER]) * inner
+        cross = pick(i, [c for _, c in OUTER]) * (1 - inner) + pick(i, [c for _, c in INNER]) * inner
+        each(cross, 1 + cross * (side - 1), lambda s: work(dist, s))
+        pl.when(i == 1)(send_maps)
+        pl.when(i == 4)(share_maps)
+        pl.when(i == 6)(low_grads)
+
+    each(0, len(OUTER), step)
+
+    def pairs(k, c):
         for sign in (-1, 1):
             z = at_line + sign * k
 
             @pl.when(on_line(z))
             def _():
-                def piece(c):
+                def piece():
                     def wait_pair(s):
                         src = z * side + other(s)
                         arrived(pair_recv.at[src, chunk(c)], pair_r.at[src, c])
@@ -447,7 +485,7 @@
                     line_send[z, chunk(c)] = total.astype(BF16)
                     line_copy(z, c).start()
 
-                each(0, CHUNKS, piece)
+                piece()
 
     def near_sum(x, total_ref):
         total_ref[...] = term[at_line * side + x].astype(F32)
@@ -466,7 +504,9 @@
         x = other(s)
         near_sum(x, acc)
         term[at_line * side + x] = acc[...].astype(BF16)
-        each(0, CHUNKS, lambda c: pair_copy(at_line, x, c).start())
+
+    def send_merged(c):
+        each(1, side, lambda s: pair_copy(at_line, other(s), c).start())
 
     def in_grads():
         def arrived_lg(s):
@@ -521,15 +561,19 @@
             go_buf[:, cols(rep)] = total.astype(BF16)
             each(1, nd, lambda s: go_copy(s).start())
 
+    for c in range(CHUNKS):
+        pairs(2, c)
+    each(1, side, merge)
+    pl.when(~outer)(lambda: each(0, CHUNKS, send_merged))
+    out_grads()
+    for c in range(CHUNKS):
+        for k in range(3, line):
+            pairs(k, c)
+        pl.when(outer)(lambda c=c: send_merged(c))
+    mate_sum()
     in_grads()
-    pairs(2)
-    out_grads()
-    each(1, side, merge)
-    for k in range(3, line):
-        pairs(k)
-    mate_sum()
-
     near_sum(at_side, acc)
+    expert_sum()
 
     def add_merged(s):
         src = at_line * side + other(s)
@@ -537,7 +581,6 @@
         acc[...] += pair_recv[src].astype(F32)
 
     each(1, side, add_merged)
-    expert_sum()
 
     for k in range(2, line):
         for sign in (-1, 1):
@@ -591,7 +634,13 @@
             def _():
                 down_copy(z, c).wait_send()
 
-            each(1, side, lambda s: side_copy(z, s, c).wait_send())
+            @pl.when(crosses(z))
+            def _():
+                each(1, side, lambda s: side_copy(z, s, c).wait_send())
+
+            @pl.when((z == at_line) & outer)
+            def _():
+                each(1, side, lambda s: onward_copy(s, c).wait_send())
 
             @pl.when((z == at_line) | (z - at_line >= 2) | (at_line - z >= 2))
             def _():
@@ -672,7 +721,7 @@
             pltpu.VMEM((2, side, rows, width), BF16),
             pltpu.VMEM((line, rows, width), BF16),
             pltpu.VMEM((line, rows, width), BF16),
-            pltpu.VMEM((n, 8, rows), F32),
+            pltpu.VMEM((n, 1, rows), F32),
             pltpu.VMEM((n, rank, width), BF16),
             pltpu.VMEM((n, rank, rows), BF16),
             pltpu.VMEM((n, rank, rows), BF16),
@@ -689,7 +738,8 @@
             dma((6,)),
         ]
         + [dma((line, CHUNKS))] * 2
-        + [dma((n, CHUNKS))] * 4
+        + [dma((n, CHUNKS)), dma((side, CHUNKS))]
+        + [dma((n, CHUNKS))] * 3
         + [dma((2, side))] * 2
         + [dma((line, CHUNKS))] * 2
         + [dma((n,))] * 4

time: 65.6 us -> 60.2 us (0.918)
  Pallas kernels: 64.8 us -> 59.4 us
    pallas_call x1, Pallas kernels: 63.1 us -> 57.7 us  [shards(): pl.pallas_call(functools.partial(kernel, n, nd), out_shape=(jax.ShapeDtyp...]
where the time goes in v2:
time: 60.2 us; the launch traced here: 60 us
  Pallas kernels  59.4 us (99%)
  between operations  0.64 us (1%)
    pallas_call x1, Pallas kernels, shards(): pl.pallas_call(functools.partial(kernel, n, nd), out_shape=(jax.ShapeDtyp...  57.7 us
    pallas_call x1, Pallas kernels, shards(): pl.pallas_call(hand_over, out_shape=tuple((jax.ShapeDtypeStruct(r.shape,...  1.7 us

profile of v2, /device:TPU:0, one launch (start us, length us, event | category | flops | bytes accessed | tf_op | source)
XLA Modules:
  0.0 60.0 jit_solution(3695918447999970056)
XLA Ops:
  0.6 57.7 %shard_map.112 = (bf16[128,1024]{1,0:T(8,128)(2,1)}, bf16[1,16,704]{2,1,0:T(8,128)(2,1)}, bf16[1,16,1024]{2,1,0:T(8,128)(2,1)}) custom-call(bf16[128,1024]{1,0:T(8,128)(2,1)} %tok_h.1, s32[6,128]{1,0:T(8,128)} %bitcast.6, f32[6,128]{1,0:T(8,128)} %bitcast.7, bf16[128,1024]{1,0:T(8,128)(2,1)} %og_ref.1, bf16[1,704,1024]{2,1,0:T(8,128)(2,1)} %bitcast.4, ...), custom_call_target="tpu_custom_call" | custom-call | tf_op jit(solution)/shard_map/pallas_call | solution.py:704
  58.4 1.7 %shard_map.113 = (bf16[128,1024]{1,0:T(8,128)(2,1)}, bf16[1,16,704]{2,1,0:T(8,128)(2,1)}, bf16[1,16,1024]{2,1,0:T(8,128)(2,1)}) custom-call(bf16[128,1024]{1,0:T(8,128)(2,1)} %get-tuple-element.6.a_ref, bf16[1,16,704]{2,1,0:T(8,128)(2,1)} %get-tuple-element.7.b_ref, bf16[1,16,1024]{2,1,0:T(8,128)(2,1)} %get-tuple-element.8.c_ref), custom_call_target="tpu_custom_call" | custom-call | tf_op jit(solution)/shard_map/pallas_call | solution.py:765

commit v3 on v2

--- a/solution.py
+++ b/solution.py
@@ -50,18 +50,22 @@
     n,
     nd,
     tok_h,
+    idx_h,
+    w_h,
+    og_h,
+    gw_h,
+    uw_h,
+    dw_h,
+    ad_h,
+    au_h,
+    mixed_h,
+    gin_h,
+    gout_h,
+    tok_all,
     idx_ref,
     w_ref,
     og_ref,
-    gw_h,
-    uw_h,
-    dw_h,
     ad_ref,
-    au_h,
-    mixed_ref,
-    gin_ref,
-    gout_ref,
-    tok_all,
     gw,
     uw,
     dw,
@@ -85,6 +89,8 @@
     go_buf,
     gin_all,
     acc,
+    mixed_ref,
+    gin_ref,
     loc_sem,
     up_s,
     down_s,
@@ -123,9 +129,9 @@
     at_line = me // side
     at_side = lax.rem(me, side)
     rows = tok_all.shape[1]
-    rank = ad_ref.shape[1]
+    rank = ad_h.shape[1]
     width = tok_all.shape[2]
-    hidden = ad_ref.shape[2]
+    hidden = ad_h.shape[2]
     parts = parts_of(nd, width)
     part = width // parts
     cr = rows // CHUNKS
@@ -177,8 +183,14 @@
         pltpu.make_async_copy(uw_h.at[0], uw, loc_sem.at[2]),
         pltpu.make_async_copy(dw_h.at[0], dw.at[pl.ds(0, hidden)], loc_sem.at[3]),
         pltpu.make_async_copy(au_h.at[0], dw.at[pl.ds(hidden, rank)], loc_sem.at[4]),
+        pltpu.make_async_copy(ad_h.at[0], ad_ref, loc_sem.at[6]),
+        pltpu.make_async_copy(og_h, og_ref, loc_sem.at[7]),
     ]
-    for load in loads:
+    tables = [
+        pltpu.make_async_copy(idx_h, idx_ref, loc_sem.at[8]),
+        pltpu.make_async_copy(w_h, w_ref, loc_sem.at[9]),
+    ]
+    for load in tables + loads:
         load.start()
 
     def load_map():
@@ -214,6 +226,8 @@
         row = jnp.sum(jnp.where(idx_ref[...] == e, w_ref[...], 0.0), axis=0, keepdims=True)
         gexp[e] = jnp.broadcast_to(row, (rank, rows))
 
+    for load in tables:
+        load.wait()
     each(0, n, spread_gates)
     gate_recv[me] = gexp[me, 0:1]
 
@@ -388,7 +402,7 @@
         g = dot_nt(x, gw[...])
         u = dot_nt(x, uw[...])
         h = (g / (1.0 + jnp.exp(-g)) * u).astype(BF16)
-        low = dot_nt(h, ad_ref[0])
+        low = dot_nt(h, ad_ref[...])
         hid_all[src, :, 0:hidden] = h
         hid_all[src, :, hidden : hidden + rank] = low.astype(BF16)
         out = dot(hid_all[src], dw[...]).astype(BF16)
@@ -563,14 +577,17 @@
 
     for c in range(CHUNKS):
         pairs(2, c)
+    out_grads()
+    for k in range(3, line):
+        pairs(k, 0)
     each(1, side, merge)
-    pl.when(~outer)(lambda: each(0, CHUNKS, send_merged))
-    out_grads()
-    for c in range(CHUNKS):
+    send_merged(0)
+    pl.when(~outer)(lambda: each(1, CHUNKS, send_merged))
+    mate_sum()
+    for c in range(1, CHUNKS):
         for k in range(3, line):
             pairs(k, c)
         pl.when(outer)(lambda c=c: send_merged(c))
-    mate_sum()
     in_grads()
     near_sum(at_side, acc)
     expert_sum()
@@ -594,13 +611,18 @@
                 acc[...] += line_recv[z].astype(F32)
 
     mixed_ref[...] = acc[...].astype(BF16)
+    put_mixed = pltpu.make_async_copy(mixed_ref, mixed_h, loc_sem.at[0])
+    put_gin = pltpu.make_async_copy(gin_ref, gin_h.at[0], loc_sem.at[1])
+    put_gout = pltpu.make_async_copy(go_buf, gout_h.at[0], loc_sem.at[2])
+    put_mixed.start()
 
     def arrived_gin(s):
         p = mate(s)
         arrived(gin_all.at[p], gin_r.at[p])
 
     each(1, nd, arrived_gin)
-    gin_ref[0] = jnp.sum(gin_all[...], axis=0)[:, 0:hidden].astype(BF16)
+    gin_ref[...] = jnp.sum(gin_all[...], axis=0)[:, 0:hidden].astype(BF16)
+    put_gin.start()
 
     def arrived_go(s):
         p = mate(s)
@@ -610,7 +632,7 @@
             arrived(go_buf.at[:, cols(p)], go_r.at[p])
 
     each(1, nd, arrived_go)
-    gout_ref[0] = go_buf[...]
+    put_gout.start()
 
     def drain(s):
         gate_copy(s).wait_send()
@@ -671,6 +693,9 @@
             go_copy(s).wait_send()
 
     each(1, nd, drain_mates)
+    put_mixed.wait()
+    put_gin.wait()
+    put_gout.wait()
 
 
 def hand_over(a_ref, b_ref, c_ref, x_ref, y_ref, z_ref):
@@ -699,7 +724,7 @@
     parts = parts_of(nd, width)
     part = width // parts
     vmem = pl.BlockSpec(memory_space=pltpu.VMEM)
-    anywhere = pl.BlockSpec(memory_space=pl.ANY)
+    hbm = pl.BlockSpec(memory_space=pltpu.HBM)
     dma = pltpu.SemaphoreType.DMA
     results = pl.pallas_call(
         functools.partial(kernel, n, nd),
@@ -708,10 +733,14 @@
             jax.ShapeDtypeStruct((1, rank, hidden), BF16),
             jax.ShapeDtypeStruct((1, rank, width), BF16),
         ),
-        in_specs=[anywhere, vmem, vmem, vmem, anywhere, anywhere, anywhere, vmem, anywhere],
-        out_specs=(vmem, vmem, vmem),
+        in_specs=[hbm] * 9,
+        out_specs=(hbm,) * 3,
         scratch_shapes=[
             pltpu.VMEM((n, rows, width), BF16),
+            pltpu.VMEM(chosen_expert_index.shape[::-1], jnp.int32),
+            pltpu.VMEM(router_gate_weight.shape[::-1], F32),
+            pltpu.VMEM((rows, width), BF16),
+            pltpu.VMEM((rank, hidden), BF16),
             pltpu.VMEM((hidden, width), BF16),
             pltpu.VMEM((hidden, width), BF16),
             pltpu.VMEM((hidden + rank, width), BF16),
@@ -735,7 +764,9 @@
             pltpu.VMEM((rank, width), BF16),
             pltpu.VMEM((nd, rank, hidden + rank), F32),
             pltpu.VMEM((rows, width), F32),
-            dma((6,)),
+            pltpu.VMEM((rows, width), BF16),
+            pltpu.VMEM((rank, hidden), BF16),
+            dma((10,)),
         ]
         + [dma((line, CHUNKS))] * 2
         + [dma((n, CHUNKS)), dma((side, CHUNKS))]

time: 60.2 us -> 58.9 us (0.978)
  Pallas kernels: 59.4 us -> 58.1 us
    pallas_call x1, Pallas kernels: 57.7 us -> 56.4 us  [shards(): pl.pallas_call(functools.partial(kernel, n, nd), out_shape=(jax.ShapeDtyp...]
where the time goes in v3:
time: 58.9 us; the launch traced here: 58.7 us
  Pallas kernels  58.1 us (99%)
  between operations  0.64 us (1%)
    pallas_call x1, Pallas kernels, shards(): pl.pallas_call(functools.partial(kernel, n, nd), out_shape=(jax.ShapeDtyp...  56.4 us
    pallas_call x1, Pallas kernels, shards(): pl.pallas_call(hand_over, out_shape=tuple((jax.ShapeDtypeStruct(r.shape,...  1.7 us

profile of v3, /device:TPU:0, one launch (start us, length us, event | category | flops | bytes accessed | tf_op | source)
XLA Modules:
  0.0 58.7 jit_solution(8666969805482950593)
XLA Ops:
  0.6 56.4 %shard_map.112 = (bf16[128,1024]{1,0:T(8,128)(2,1)}, bf16[1,16,704]{2,1,0:T(8,128)(2,1)}, bf16[1,16,1024]{2,1,0:T(8,128)(2,1)}) custom-call(bf16[128,1024]{1,0:T(8,128)(2,1)} %tok_h.1, s32[6,128]{1,0:T(8,128)} %bitcast.6, f32[6,128]{1,0:T(8,128)} %bitcast.7, bf16[128,1024]{1,0:T(8,128)(2,1)} %og_h.1, bf16[1,704,1024]{2,1,0:T(8,128)(2,1)} %bitcast.4, ...), custom_call_target="tpu_custom_call" | custom-call | tf_op jit(solution)/shard_map/pallas_call | solution.py:729
  57.0 1.7 %shard_map.113 = (bf16[128,1024]{1,0:T(8,128)(2,1)}, bf16[1,16,704]{2,1,0:T(8,128)(2,1)}, bf16[1,16,1024]{2,1,0:T(8,128)(2,1)}) custom-call(bf16[128,1024]{1,0:T(8,128)(2,1)} %get-tuple-element.6.a_ref, bf16[1,16,704]{2,1,0:T(8,128)(2,1)} %get-tuple-element.7.b_ref, bf16[1,16,1024]{2,1,0:T(8,128)(2,1)} %get-tuple-element.8.c_ref), custom_call_target="tpu_custom_call" | custom-call | tf_op jit(solution)/shard_map/pallas_call | solution.py:796

commit v4 on v3

--- a/solution.py
+++ b/solution.py
@@ -35,8 +35,8 @@
 
 
 OUTER = ((0, 0), (1, 0), (0, 1), (2, 0), (1, 1), (2, 1), (3, 0), (3, 1))
-INNER = ((0, 0), (1, 0), (-1, 0), (0, 1), (1, 1), (-1, 1), (2, 1), (2, 0))
-RELAYS = {1: ((1, 0), (1, 1)), 2: ((2, 0),), 3: ((2, 1),), 5: ((3, 0), (3, 1))}
+INNER = ((0, 0), (1, 0), (-1, 0), (0, 1), (1, 1), (2, 0), (2, 1), (-1, 1))
+RELAYS = {1: ((1, 0), (1, 1)), 2: ((2, 0),), 3: ((2, 1),), 4: ((3, 0),), 5: ((3, 1),)}
 
 
 def parts_of(nd, width):
@@ -91,6 +91,7 @@
     acc,
     mixed_ref,
     gin_ref,
+    meet_sem,
     loc_sem,
     up_s,
     down_s,
@@ -203,13 +204,17 @@
         load_map().start()
 
     barrier = pltpu.get_barrier_semaphore()
-    each(
-        1,
-        n,
-        lambda s: pl.semaphore_signal(
-            barrier, inc=1, device_id={"expert": peer(s)}, device_id_type=MESH
-        ),
-    )
+
+    def greet(sem, p):
+        pl.semaphore_signal(sem, inc=1, device_id={"expert": p}, device_id_type=MESH)
+
+    def greet_sides(sem):
+        each(1, side, lambda s: greet(sem, at_line * side + other(s)))
+
+    above, below = at_line + 1 < line, at_line >= 1
+    greet_sides(barrier)
+    pl.when(above)(lambda: greet(barrier, me + side))
+    pl.when(below)(lambda: greet(barrier, me - side))
     each(
         1,
         nd,
@@ -325,6 +330,9 @@
     def arrived_tok(k, c):
         arrived(tok_all.at[k, chunk(c)], tok_r.at[k, c])
 
+    def far(a, b):
+        return (a - b >= 2) | (b - a >= 2)
+
     def crosses(z):
         return outer | (z != at_line - front)
 
@@ -342,9 +350,18 @@
             down_copy(z, c).start()
 
     loads[0].wait()
-    pl.semaphore_wait(barrier, n - 1 + nd - 1)
-
-    each(1, n, lambda s: gate_copy(s).start())
+    neighbours = side - 1 + above.astype(jnp.int32) + below.astype(jnp.int32)
+    pl.semaphore_wait(barrier, neighbours + nd - 1)
+
+    def meet_all():
+        pl.when(below)(lambda: pl.semaphore_wait(meet_sem.at[0], 1))
+        pl.when(above)(lambda: greet(meet_sem.at[0], me + side))
+        pl.when(above)(lambda: pl.semaphore_wait(meet_sem.at[1], 1))
+        pl.when(below)(lambda: greet(meet_sem.at[1], me - side))
+        greet_sides(meet_sem.at[2])
+        pl.semaphore_wait(meet_sem.at[2], side - 1)
+        each(1, n, lambda s: gate_copy(s).start())
+
     each(0, CHUNKS, lambda c: spread(at_line, c, True, True))
     for load in loads[1:]:
         load.wait()
@@ -436,13 +453,19 @@
                 rk_send[src] = low_t
                 rk_copy(src).start()
 
-            @pl.when((s > 0) & ((dist == 1) | (dist == -1)))
+            @pl.when((s > 0) & (dist == 1))
             def _():
                 near_copy(z, x).start()
 
+            last = jnp.where(outer & (dist == 2), 1, CHUNKS)
+
             @pl.when((s > 0) & (dist >= 2))
             def _():
-                each(0, CHUNKS, lambda c: pair_copy(z, x, c).start())
+                each(0, last, lambda c: pair_copy(z, x, c).start())
+
+            @pl.when((s > 0) & (dist == 3))
+            def _():
+                each(1, CHUNKS, lambda c: pair_copy(z - front, x, c).start())
 
         run()
 
@@ -450,6 +473,27 @@
         @pl.when(on_line(z))
         def _():
             near_copy(z, at_side).start()
+
+    def near_sum(x, total_ref):
+        total_ref[...] = term[at_line * side + x].astype(F32)
+
+        @pl.when((at_line >= 1) & (2 * (at_line - 1) < line))
+        def _():
+            arrived(near_recv.at[0, x], near_r.at[0, x])
+            total_ref[...] += near_recv[0, x].astype(F32)
+
+        @pl.when((at_line + 1 < line) & (2 * (at_line + 1) >= line))
+        def _():
+            arrived(near_recv.at[1, x], near_r.at[1, x])
+            total_ref[...] += near_recv[1, x].astype(F32)
+
+    def merge(s):
+        x = other(s)
+        near_sum(x, acc)
+        term[at_line * side + x] = acc[...].astype(BF16)
+
+    def send_merged(c):
+        each(1, side, lambda s: pair_copy(at_line, other(s), c).start())
 
     def pick(i, values):
         total = 0
@@ -466,61 +510,38 @@
                     relay(k, c)
 
         pl.when(i == 3)(lambda: near_own(at_line + front))
-        pl.when(i == 5)(lambda: near_own(at_line - front))
+        pl.when((i == 7) & outer)(lambda: send_merged(0))
         inner = 1 - outer.astype(jnp.int32)
         dist = pick(i, [d for d, _ in OUTER]) * (1 - inner) + pick(i, [d for d, _ in INNER]) * inner
         cross = pick(i, [c for _, c in OUTER]) * (1 - inner) + pick(i, [c for _, c in INNER]) * inner
         each(cross, 1 + cross * (side - 1), lambda s: work(dist, s))
+        pl.when(i == 0)(meet_all)
         pl.when(i == 1)(send_maps)
         pl.when(i == 4)(share_maps)
         pl.when(i == 6)(low_grads)
 
     each(0, len(OUTER), step)
 
-    def pairs(k, c):
-        for sign in (-1, 1):
-            z = at_line + sign * k
-
-            @pl.when(on_line(z))
-            def _():
-                def piece():
-                    def wait_pair(s):
-                        src = z * side + other(s)
-                        arrived(pair_recv.at[src, chunk(c)], pair_r.at[src, c])
-
-                    each(1, side, wait_pair)
-
-                    def add(s, total):
-                        return total + pair_recv[z * side + other(s), chunk(c)].astype(F32)
-
-                    total = lax.fori_loop(
-                        1, side, add, term[z * side + at_side, chunk(c)].astype(F32)
-                    )
-                    line_send[z, chunk(c)] = total.astype(BF16)
-                    line_copy(z, c).start()
-
-                piece()
-
-    def near_sum(x, total_ref):
-        total_ref[...] = term[at_line * side + x].astype(F32)
-
-        @pl.when(at_line >= 1)
-        def _():
-            arrived(near_recv.at[0, x], near_r.at[0, x])
-            total_ref[...] += near_recv[0, x].astype(F32)
-
-        @pl.when(at_line + 1 < line)
-        def _():
-            arrived(near_recv.at[1, x], near_r.at[1, x])
-            total_ref[...] += near_recv[1, x].astype(F32)
-
-    def merge(s):
-        x = other(s)
-        near_sum(x, acc)
-        term[at_line * side + x] = acc[...].astype(BF16)
-
-    def send_merged(c):
-        each(1, side, lambda s: pair_copy(at_line, other(s), c).start())
+    def pairs(dist, c):
+        z = at_line + front * dist
+
+        @pl.when(on_line(z))
+        def _():
+            def wait_pair(s):
+                src = z * side + other(s)
+                arrived(pair_recv.at[src, chunk(c)], pair_r.at[src, c])
+
+            each(1, side, wait_pair)
+
+            def add(s, total):
+                return total + pair_recv[z * side + other(s), chunk(c)].astype(F32)
+
+            total = lax.fori_loop(1, side, add, term[z * side + at_side, chunk(c)].astype(F32))
+            line_send[z, chunk(c)] = total.astype(BF16)
+            line_copy(z, c).start()
+
+    def late_pairs(c):
+        pairs(jnp.where(outer, line - 1, -1), c)
 
     def in_grads():
         def arrived_lg(s):
@@ -575,19 +596,20 @@
             go_buf[:, cols(rep)] = total.astype(BF16)
             each(1, nd, lambda s: go_copy(s).start())
 
-    for c in range(CHUNKS):
-        pairs(2, c)
+    def send_back(s):
+        each(0, CHUNKS, lambda c: pair_copy(at_line - front, other(s), c).start())
+
+    pairs(2, 0)
+    pl.when(~outer)(lambda: each(1, side, send_back))
+    pl.when(~outer)(lambda: each(1, CHUNKS, lambda c: pairs(2, c)))
     out_grads()
-    for k in range(3, line):
-        pairs(k, 0)
-    each(1, side, merge)
-    send_merged(0)
-    pl.when(~outer)(lambda: each(1, CHUNKS, send_merged))
+    late_pairs(0)
     mate_sum()
-    for c in range(1, CHUNKS):
-        for k in range(3, line):
-            pairs(k, c)
-        pl.when(outer)(lambda c=c: send_merged(c))
+    each(1, CHUNKS, late_pairs)
+    pl.when(outer)(lambda: each(1, CHUNKS, lambda c: pairs(2, c)))
+    pl.when(outer)(lambda: each(1, CHUNKS, send_merged))
+    pl.when(~outer)(lambda: each(1, side, merge))
+    pl.when(~outer)(lambda: each(0, CHUNKS, send_merged))
     in_grads()
     near_sum(at_side, acc)
     expert_sum()
@@ -599,17 +621,13 @@
 
     each(1, side, add_merged)
 
-    for k in range(2, line):
-        for sign in (-1, 1):
-            z = at_line + sign * k
-
-            @pl.when(on_line(z))
-            def _():
-                each(
-                    0, CHUNKS, lambda c: arrived(line_recv.at[z, chunk(c)], line_r.at[z, c])
-                )
-                acc[...] += line_recv[z].astype(F32)
-
+    def add_line(z):
+        @pl.when(far(at_line, z) | (outer & (z == at_line + front)))
+        def _():
+            each(0, CHUNKS, lambda c: arrived(line_recv.at[z, chunk(c)], line_r.at[z, c]))
+            acc[...] += line_recv[z].astype(F32)
+
+    each(0, line, add_line)
     mixed_ref[...] = acc[...].astype(BF16)
     put_mixed = pltpu.make_async_copy(mixed_ref, mixed_h, loc_sem.at[0])
     put_gin = pltpu.make_async_copy(gin_ref, gin_h.at[0], loc_sem.at[1])
@@ -664,17 +682,19 @@
             def _():
                 each(1, side, lambda s: onward_copy(s, c).wait_send())
 
-            @pl.when((z == at_line) | (z - at_line >= 2) | (at_line - z >= 2))
+            lined = far(at_line, z) | (~outer & (z == at_line - front))
+
+            @pl.when((z == at_line) | lined)
             def _():
                 each(1, side, lambda s: pair_copy(z, other(s), c).wait_send())
 
-            @pl.when((z - at_line >= 2) | (at_line - z >= 2))
+            @pl.when(lined)
             def _():
                 line_copy(z, c).wait_send()
 
         each(0, CHUNKS, piece)
 
-        @pl.when((z - at_line == 1) | (at_line - z == 1))
+        @pl.when(z == at_line + front)
         def _():
             each(0, side, lambda x: near_copy(z, x).wait_send())
 
@@ -766,6 +786,7 @@
             pltpu.VMEM((rows, width), F32),
             pltpu.VMEM((rows, width), BF16),
             pltpu.VMEM((rank, hidden), BF16),
+            pltpu.SemaphoreType.REGULAR((3,)),
             dma((10,)),
         ]
         + [dma((line, CHUNKS))] * 2

time: 58.9 us -> 57.1 us (0.969)
  Pallas kernels: 58.1 us -> 56.3 us
    pallas_call x1, Pallas kernels: 56.4 us -> 54.6 us  [shards(): pl.pallas_call(functools.partial(kernel, n, nd), out_shape=(jax.ShapeDtyp...]
where the time goes in v4:
time: 57.1 us; the launch traced here: 57 us
  Pallas kernels  56.3 us (99%)
  between operations  0.64 us (1%)
    pallas_call x1, Pallas kernels, shards(): pl.pallas_call(functools.partial(kernel, n, nd), out_shape=(jax.ShapeDtyp...  54.6 us
    pallas_call x1, Pallas kernels, shards(): pl.pallas_call(hand_over, out_shape=tuple((jax.ShapeDtypeStruct(r.shape,...  1.7 us

profile of v4, /device:TPU:0, one launch (start us, length us, event | category | flops | bytes accessed | tf_op | source)
XLA Modules:
  0.0 57.0 jit_solution(3443438652932233334)
XLA Ops:
  0.6 54.6 %shard_map.112 = (bf16[128,1024]{1,0:T(8,128)(2,1)}, bf16[1,16,704]{2,1,0:T(8,128)(2,1)}, bf16[1,16,1024]{2,1,0:T(8,128)(2,1)}) custom-call(bf16[128,1024]{1,0:T(8,128)(2,1)} %tok_h.1, s32[6,128]{1,0:T(8,128)} %bitcast.6, f32[6,128]{1,0:T(8,128)} %bitcast.7, bf16[128,1024]{1,0:T(8,128)(2,1)} %og_h.1, bf16[1,704,1024]{2,1,0:T(8,128)(2,1)} %bitcast.4, ...), custom_call_target="tpu_custom_call" | custom-call | tf_op jit(solution)/shard_map/pallas_call | solution.py:749
  55.3 1.7 %shard_map.113 = (bf16[128,1024]{1,0:T(8,128)(2,1)}, bf16[1,16,704]{2,1,0:T(8,128)(2,1)}, bf16[1,16,1024]{2,1,0:T(8,128)(2,1)}) custom-call(bf16[128,1024]{1,0:T(8,128)(2,1)} %get-tuple-element.6.a_ref, bf16[1,16,704]{2,1,0:T(8,128)(2,1)} %get-tuple-element.7.b_ref, bf16[1,16,1024]{2,1,0:T(8,128)(2,1)} %get-tuple-element.8.c_ref), custom_call_target="tpu_custom_call" | custom-call | tf_op jit(solution)/shard_map/pallas_call | solution.py:817

commit v5 on v4

--- a/solution.py
+++ b/solution.py
@@ -231,10 +231,6 @@
         row = jnp.sum(jnp.where(idx_ref[...] == e, w_ref[...], 0.0), axis=0, keepdims=True)
         gexp[e] = jnp.broadcast_to(row, (rank, rows))
 
-    for load in tables:
-        load.wait()
-    each(0, n, spread_gates)
-    gate_recv[me] = gexp[me, 0:1]
 
     def up_copy(z, c):
         k = z * side + at_side
@@ -363,6 +359,10 @@
         each(1, n, lambda s: gate_copy(s).start())
 
     each(0, CHUNKS, lambda c: spread(at_line, c, True, True))
+    for load in tables:
+        load.wait()
+    each(0, n, spread_gates)
+    gate_recv[me] = gexp[me, 0:1]
     for load in loads[1:]:
         load.wait()
 
@@ -599,8 +599,8 @@
     def send_back(s):
         each(0, CHUNKS, lambda c: pair_copy(at_line - front, other(s), c).start())
 
+    pl.when(~outer)(lambda: each(1, side, send_back))
     pairs(2, 0)
-    pl.when(~outer)(lambda: each(1, side, send_back))
     pl.when(~outer)(lambda: each(1, CHUNKS, lambda c: pairs(2, c)))
     out_grads()
     late_pairs(0)

time: 57.1 us -> 56.5 us (0.989)
  Pallas kernels: 56.3 us -> 55.6 us
    pallas_call x1, Pallas kernels: 54.6 us -> 53.9 us  [shards(): pl.pallas_call(functools.partial(kernel, n, nd), out_shape=(jax.ShapeDtyp...]
where the time goes in v5:
time: 56.5 us; the launch traced here: 56.2 us
  Pallas kernels  55.6 us (98%)
  between operations  0.64 us (1%)
    pallas_call x1, Pallas kernels, shards(): pl.pallas_call(functools.partial(kernel, n, nd), out_shape=(jax.ShapeDtyp...  53.9 us
    pallas_call x1, Pallas kernels, shards(): pl.pallas_call(hand_over, out_shape=tuple((jax.ShapeDtypeStruct(r.shape,...  1.7 us

profile of v5, /device:TPU:0, one launch (start us, length us, event | category | flops | bytes accessed | tf_op | source)
XLA Modules:
  0.0 56.2 jit_solution(9465051875577141366)
XLA Ops:
  0.6 53.9 %shard_map.112 = (bf16[128,1024]{1,0:T(8,128)(2,1)}, bf16[1,16,704]{2,1,0:T(8,128)(2,1)}, bf16[1,16,1024]{2,1,0:T(8,128)(2,1)}) custom-call(bf16[128,1024]{1,0:T(8,128)(2,1)} %tok_h.1, s32[6,128]{1,0:T(8,128)} %bitcast.6, f32[6,128]{1,0:T(8,128)} %bitcast.7, bf16[128,1024]{1,0:T(8,128)(2,1)} %og_h.1, bf16[1,704,1024]{2,1,0:T(8,128)(2,1)} %bitcast.4, ...), custom_call_target="tpu_custom_call" | custom-call | tf_op jit(solution)/shard_map/pallas_call | solution.py:749
  54.5 1.7 %shard_map.113 = (bf16[128,1024]{1,0:T(8,128)(2,1)}, bf16[1,16,704]{2,1,0:T(8,128)(2,1)}, bf16[1,16,1024]{2,1,0:T(8,128)(2,1)}) custom-call(bf16[128,1024]{1,0:T(8,128)(2,1)} %get-tuple-element.6.a_ref, bf16[1,16,704]{2,1,0:T(8,128)(2,1)} %get-tuple-element.7.b_ref, bf16[1,16,1024]{2,1,0:T(8,128)(2,1)} %get-tuple-element.8.c_ref), custom_call_target="tpu_custom_call" | custom-call | tf_op jit(solution)/shard_map/pallas_call | solution.py:817

commit v6 on v5

--- a/solution.py
+++ b/solution.py
@@ -603,13 +603,13 @@
     pairs(2, 0)
     pl.when(~outer)(lambda: each(1, CHUNKS, lambda c: pairs(2, c)))
     out_grads()
+    pl.when(~outer)(lambda: each(1, side, merge))
+    pl.when(~outer)(lambda: send_merged(0))
     late_pairs(0)
     mate_sum()
     each(1, CHUNKS, late_pairs)
     pl.when(outer)(lambda: each(1, CHUNKS, lambda c: pairs(2, c)))
-    pl.when(outer)(lambda: each(1, CHUNKS, send_merged))
-    pl.when(~outer)(lambda: each(1, side, merge))
-    pl.when(~outer)(lambda: each(0, CHUNKS, send_merged))
+    each(1, CHUNKS, send_merged)
     in_grads()
     near_sum(at_side, acc)
     expert_sum()

time: 56.5 us -> 56.5 us (level)
  no operation moved by 1% of the time
where the time goes in v6:
time: 56.5 us; the launch traced here: 56.2 us
  Pallas kernels  55.6 us (98%)
  between operations  0.64 us (1%)
    pallas_call x1, Pallas kernels, shards(): pl.pallas_call(functools.partial(kernel, n, nd), out_shape=(jax.ShapeDtyp...  53.9 us
    pallas_call x1, Pallas kernels, shards(): pl.pallas_call(hand_over, out_shape=tuple((jax.ShapeDtypeStruct(r.shape,...  1.7 us

profile of v6, /device:TPU:0, one launch (start us, length us, event | category | flops | bytes accessed | tf_op | source)
XLA Modules:
  0.0 56.2 jit_solution(5624655881252170713)
XLA Ops:
  0.6 53.9 %shard_map.112 = (bf16[128,1024]{1,0:T(8,128)(2,1)}, bf16[1,16,704]{2,1,0:T(8,128)(2,1)}, bf16[1,16,1024]{2,1,0:T(8,128)(2,1)}) custom-call(bf16[128,1024]{1,0:T(8,128)(2,1)} %tok_h.1, s32[6,128]{1,0:T(8,128)} %bitcast.6, f32[6,128]{1,0:T(8,128)} %bitcast.7, bf16[128,1024]{1,0:T(8,128)(2,1)} %og_h.1, bf16[1,704,1024]{2,1,0:T(8,128)(2,1)} %bitcast.4, ...), custom_call_target="tpu_custom_call" | custom-call | tf_op jit(solution)/shard_map/pallas_call | solution.py:749
  54.5 1.7 %shard_map.113 = (bf16[128,1024]{1,0:T(8,128)(2,1)}, bf16[1,16,704]{2,1,0:T(8,128)(2,1)}, bf16[1,16,1024]{2,1,0:T(8,128)(2,1)}) custom-call(bf16[128,1024]{1,0:T(8,128)(2,1)} %get-tuple-element.6.a_ref, bf16[1,16,704]{2,1,0:T(8,128)(2,1)} %get-tuple-element.7.b_ref, bf16[1,16,1024]{2,1,0:T(8,128)(2,1)} %get-tuple-element.8.c_ref), custom_call_target="tpu_custom_call" | custom-call | tf_op jit(solution)/shard_map/pallas_call | solution.py:817
